TPU v7x, 32 devices: a whole 2x2x4 slice. The times are simulated.
32 devices in a mesh: gx: 4 (over y, x), gy: 4 (over z), gz: 2 (over core).
Axes of the slice: x: 2, y: 2, z: 4, core: 2. Of those that a mesh axis runs over, the one named last changes fastest.
Arguments:
- fields: bfloat16 [4096, 2048], P(('gx', 'gy', 'gz')), may hold values from -6 to 6
- coordinates: float32 [3, 524288], P(None, ('gx', 'gy', 'gz')), may hold values from -1 to 1
- element_rank: int32 [524288, 1], P(('gx', 'gy', 'gz')), may hold values from 0 to 31; in each aligned block of 16384 rows (0 to 16383, 16384 to 32767, ...) at most 640 rows name the same one
- element_slot: int32 [524288], P(('gx', 'gy', 'gz')), may hold values from 0 to 127
Outputs:
- samples: float32 [4, 524288], P(None, ('gx', 'gy', 'gz'))
Inputs may be any that keep to these rules, and one draw needn't show every extreme that they name: `element_rank`: among the probes of one device no rank is named by more than 640 probes, and in some devices' blocks one rank is named by exactly 640.
All inputs are finite; a program needn't handle non-finite values.
Results may differ from a plain program's by a relative error of at most 0.0024.
Values sent between devices are 32-bit elements; how exact they have to be, the bound alone decides.
A program may use at most 64 MiB of HBM per device.

v0:
```python
import functools

import jax
import jax.numpy as jnp
import numpy as np
from jax import lax
from jax.experimental import pallas as pl
from jax.experimental.pallas import tpu as pltpu
from jax.sharding import PartitionSpec as P

AXES = ("gx", "gy", "gz")
F32, BF16 = jnp.float32, jnp.bfloat16
LANES = 128
CHUNK = 256
GROUP = 4

gll_points = np.array(
    [
        -1.0,
        -0.8717401485096066,
        -0.5917001814331423,
        -0.2092992179024789,
        0.2092992179024789,
        0.5917001814331423,
        0.8717401485096066,
        1.0,
    ]
)
gll_scale = np.array(
    [1.0 / np.prod([gll_points[a] - gll_points[b] for b in range(8) if b != a]) for a in range(8)]
)
node_table = np.stack(
    [gll_scale] + [np.roll(gll_points, -k) for k in range(1, 8)], axis=0
).reshape(64, 1)


def iota_bf16(shape):
    return lax.broadcasted_iota(jnp.int32, shape, 0).astype(F32).astype(BF16)


def spread(row, count):
    return jnp.broadcast_to(row, (count, row.shape[1])).astype(BF16)


def route(count, blocks, rank_ref, coords_ref, slot_ref, prefix_ref, send_ref, row_ref, lane_ref, acc_ref):
    probes = rank_ref.shape[1]
    group = max(1, CHUNK // count)
    targets = lax.broadcasted_iota(jnp.int32, (count, CHUNK), 0)

    def place(step, carry):
        masks, hots, ranks = [], [], []
        for g in range(group):
            at = pl.ds(pl.multiple_of((step * group + g) * CHUNK, CHUNK), CHUNK)
            rank = rank_ref[:, at]
            mask = targets == jnp.broadcast_to(rank, (count, CHUNK))
            masks.append(mask)
            hots.append(jnp.where(mask, 1.0, 0.0).astype(BF16))
            ranks.append(rank.astype(F32))
        counted = jnp.dot(jnp.concatenate(hots, axis=0), prefix_ref[...], preferred_element_type=F32)
        for g in range(group):
            at = pl.ds(pl.multiple_of((step * group + g) * CHUNK, CHUNK), CHUNK)
            piece = counted[g * count : (g + 1) * count]
            place_in = jnp.where(masks[g], piece[:, :CHUNK] + carry, 0.0)
            position = jnp.sum(place_in, axis=0, keepdims=True) - 1.0
            block = jnp.floor(position * (1.0 / LANES))
            lane_ref[:, at] = position - block * LANES
            row_ref[:, at] = block * count + ranks[g]
            carry = carry + piece[:, CHUNK:]
        return carry

    lax.fori_loop(0, probes // (CHUNK * group), place, jnp.zeros((count, CHUNK), F32))

    rows = count * blocks
    part_lanes = LANES // 2
    row_ids = iota_bf16((rows, CHUNK))
    lane_ids = iota_bf16((part_lanes, CHUNK))
    one, zero = jnp.ones((), BF16), jnp.zeros((), BF16)
    acc_ref[...] = jnp.zeros_like(acc_ref)

    def scatter(step, _):
        row_hots, lane_parts = [], []
        for g in range(4):
            at = pl.ds(pl.multiple_of((step * 4 + g) * CHUNK, CHUNK), CHUNK)
            row, lane = row_ref[:, at], lane_ref[:, at]
            upper = lane >= float(part_lanes)
            halves = [jnp.where(upper, -1.0, row), jnp.where(upper, row, -1.0)]
            row_hots.append(
                jnp.concatenate([jnp.where(row_ids == spread(part, rows), one, zero) for part in halves], axis=0)
            )
            here = lane_ids == spread(jnp.where(upper, lane - float(part_lanes), lane), part_lanes)
            parts = []
            for v in range(3):
                value = coords_ref[v : v + 1, at]
                high = value.astype(BF16).astype(F32)
                parts += [high, value - high]
            parts.append(slot_ref[:, at].astype(F32))
            chosen = [jnp.where(here, spread(part, part_lanes), zero) for part in parts]
            chosen.append(jnp.zeros((part_lanes, CHUNK), BF16))
            lane_parts.append(jnp.concatenate(chosen, axis=0))
        acc_ref[...] += lax.dot_general(
            jnp.concatenate(row_hots, axis=1),
            jnp.concatenate(lane_parts, axis=1),
            (((1,), (1,)), ((), ())),
            preferred_element_type=F32,
        )
        return 0

    lax.fori_loop(0, probes // (4 * CHUNK), scatter, 0)
    left = lax.broadcasted_iota(jnp.int32, (count, LANES), 1) < part_lanes
    for b in range(blocks):
        for v in range(4):
            sides = []
            for h in range(2):
                first = h * rows + b * count
                both = acc_ref[first : first + count, v * LANES : (v + 1) * LANES]
                sides.append(both + pltpu.roll(both, part_lanes, 1))
            send_ref[v * blocks + b] = jnp.where(left, sides[0], sides[1])


def lagrange(coord, nodes_ref):
    weight = nodes_ref[0:8, :]
    spread_coord = jnp.broadcast_to(coord, (8, LANES))
    for k in range(1, 8):
        weight = weight * (spread_coord - nodes_ref[8 * k : 8 * k + 8, :])
    return weight


def interpolate(blocks, block, sources, recv_ref, fields_ref, nodes_ref, values_ref, picker_ref):
    depth = fields_ref.shape[1]
    elements = depth // 8
    zero = jnp.zeros((), BF16)
    ids = iota_bf16((16, LANES))
    weights = []
    for j, source in enumerate(sources):
        r, s, t, slot = [recv_ref[v * blocks + block, pl.ds(source, 1), :] for v in range(4)]
        weights.append((lagrange(r, nodes_ref), lagrange(s, nodes_ref)))
        weight_t = lagrange(t, nodes_ref)
        columns = slice(j * LANES, (j + 1) * LANES)
        masks = [ids == spread(slot - float(16 * k), 16) for k in range(elements // 16)]
        for c in range(8):
            weight = spread(weight_t[c : c + 1, :], 16)
            for k in range(elements // 16):
                at = c * elements + k * 16
                picker_ref[at : at + 16, columns] = jnp.where(masks[k], weight, zero)
    along = jnp.dot(fields_ref[...], picker_ref[...], preferred_element_type=F32)
    for j, source in enumerate(sources):
        weight_r, weight_s = weights[j]
        columns = slice(j * LANES, (j + 1) * LANES)
        factors = [jnp.broadcast_to(weight_r[a : a + 1, :], (8, LANES)) for a in range(8)]
        for f in range(4):
            total = along[f * 64 : f * 64 + 8, columns] * factors[0]
            for a in range(1, 8):
                total += along[f * 64 + a * 8 : f * 64 + a * 8 + 8, columns] * factors[a]
            values_ref[f * blocks + block, pl.ds(source, 1), :] = jnp.sum(
                total * weight_s, axis=0, keepdims=True
            )


def sample_kernel(
    sizes,
    blocks,
    rank_ref,
    coords_ref,
    slot_ref,
    prefix_ref,
    fields_ref,
    nodes_ref,
    back_ref,
    row_ref,
    lane_ref,
    acc_ref,
    send_ref,
    recv_ref,
    values_ref,
    picker_even,
    picker_odd,
    out_sem,
    in_sem,
    back_out_sem,
    back_in_sem,
    own_sem,
):
    count = sizes[0] * sizes[1] * sizes[2]
    me = (lax.axis_index("gx") * sizes[1] + lax.axis_index("gy")) * sizes[2] + lax.axis_index("gz")
    mesh_ids = pl.DeviceIdType.MESH

    def coordinates_of(device):
        return (device // (sizes[1] * sizes[2]), (device // sizes[2]) % sizes[1], device % sizes[2])

    def each(first, last, act):
        def body(step, _):
            act(step)
            return 0

        lax.fori_loop(first, last, body, 0)

    def behind(step):
        return lax.rem(me + count - step, count)

    def outward(step):
        other = lax.rem(me + step, count)
        return pltpu.make_async_remote_copy(
            src_ref=send_ref.at[:, other],
            dst_ref=recv_ref.at[:, me],
            send_sem=out_sem.at[step],
            recv_sem=in_sem.at[step],
            device_id=coordinates_of(other),
            device_id_type=mesh_ids,
        )

    def backward(step):
        other = behind(step)
        return pltpu.make_async_remote_copy(
            src_ref=values_ref.at[:, other],
            dst_ref=back_ref.at[:, me],
            send_sem=back_out_sem.at[step],
            recv_sem=back_in_sem.at[step],
            device_id=coordinates_of(other),
            device_id_type=mesh_ids,
        )

    barrier = pltpu.get_barrier_semaphore()
    each(
        1,
        count,
        lambda step: pl.semaphore_signal(
            barrier, inc=1, device_id=coordinates_of(lax.rem(me + step, count)), device_id_type=mesh_ids
        ),
    )
    route(count, blocks, rank_ref, coords_ref, slot_ref, prefix_ref, send_ref, row_ref, lane_ref, acc_ref)
    pl.semaphore_wait(barrier, count - 1)
    each(1, count, lambda step: outward(step).start())
    own = pltpu.make_async_copy(send_ref.at[:, me], recv_ref.at[:, me], own_sem.at[0])
    own.start()
    own.wait()
    own_back = pltpu.make_async_copy(values_ref.at[:, me], back_ref.at[:, me], own_sem.at[1])
    pickers = [picker_even, picker_odd]

    def reply(group):
        for j in range(GROUP):
            step = group * GROUP + j
            if j == 0:

                @pl.when(step == 0)
                def _():
                    own_back.start()

                @pl.when(step > 0)
                def _():
                    backward(step).start()

            else:
                backward(step).start()

    def body(group, _):
        sources = []
        for j in range(GROUP):
            step = group * GROUP + j
            if j == 0:

                @pl.when(step > 0)
                def _():
                    outward(step).wait_recv()

            else:
                outward(step).wait_recv()
            sources.append(behind(step))
        for block in range(blocks):
            interpolate(blocks, block, sources, recv_ref, fields_ref, nodes_ref, values_ref, pickers[block % 2])

        @pl.when(group > 0)
        def _():
            reply(group - 1)

        return 0

    groups = count // GROUP
    lax.fori_loop(0, groups, body, 0)
    each(1, count, lambda step: outward(step).wait_send())
    reply(groups - 1)
    each(1, count, lambda step: backward(step).wait())
    own_back.wait()


def return_kernel(blocks, values_ref, row_ref, lane_ref, out_ref, table_ref):
    probes = row_ref.shape[1]
    count = values_ref.shape[1]
    rows = blocks * count
    for f in range(4):
        table = jnp.concatenate([values_ref[f * blocks + b] for b in range(blocks)], axis=0)
        table_ref[f * LANES : (f + 1) * LANES, :] = table.T.astype(BF16)
    row_ids = iota_bf16((rows, CHUNK))
    lane_ids = lax.broadcasted_iota(jnp.int32, (LANES, CHUNK), 0).astype(F32)

    def body(step, _):
        for g in range(4):
            at = pl.ds(pl.multiple_of((step * 4 + g) * CHUNK, CHUNK), CHUNK)
            hot = jnp.where(row_ids == spread(row_ref[:, at], rows), jnp.ones((), BF16), jnp.zeros((), BF16))
            picked = jnp.dot(table_ref[...], hot, preferred_element_type=F32)
            here = lane_ids == jnp.broadcast_to(lane_ref[:, at], (LANES, CHUNK))
            for f in range(4):
                out_ref[f : f + 1, at] = jnp.sum(
                    jnp.where(here, picked[f * LANES : (f + 1) * LANES], 0.0), axis=0, keepdims=True
                )
        return 0

    lax.fori_loop(0, probes // (4 * CHUNK), body, 0)


VMEM = pl.BlockSpec(memory_space=pltpu.VMEM)


def call(kernel, inputs, outputs, scratch, **options):
    return pl.pallas_call(
        kernel,
        out_shape=outputs,
        in_specs=[VMEM] * inputs,
        out_specs=jax.tree.map(lambda _: VMEM, outputs),
        scratch_shapes=scratch,
        compiler_params=pltpu.CompilerParams(vmem_limit_bytes=48 << 20, **options),
    )


def local(sizes, fields, coordinates, element_rank, element_slot):
    count = sizes[0] * sizes[1] * sizes[2]
    probes = element_slot.shape[0]
    elements = fields.shape[0]
    capacity = 5 * probes // (4 * count)
    blocks = -(-capacity // LANES)
    layout = jax.ShapeDtypeStruct((4 * blocks, count, LANES), F32)
    line = jax.ShapeDtypeStruct((1, probes), F32)

    lower = np.arange(CHUNK)
    prefix = np.concatenate([lower[:, None] <= lower[None, :], np.ones((CHUNK, CHUNK))], axis=1)
    turned = fields.reshape(elements, 256, 8).transpose(1, 2, 0).reshape(256, 8 * elements)
    nodes = jnp.broadcast_to(jnp.asarray(node_table, F32), (64, LANES))
    picker = pltpu.VMEM((8 * elements, GROUP * LANES), BF16)
    buffer = pltpu.VMEM(layout.shape, F32)
    arrivals = pltpu.SemaphoreType.DMA((count,))
    returned, row, lane = call(
        functools.partial(sample_kernel, sizes, blocks),
        6,
        (layout, line, line),
        [pltpu.VMEM((2 * count * blocks, 4 * LANES), F32)]
        + [buffer] * 3
        + [picker] * 2
        + [arrivals] * 4
        + [pltpu.SemaphoreType.DMA((2,))],
        collective_id=0,
        has_side_effects=True,
    )(
        element_rank.reshape(1, probes),
        coordinates,
        element_slot.reshape(1, probes),
        jnp.asarray(prefix, BF16),
        turned,
        nodes,
    )
    return call(
        functools.partial(return_kernel, blocks),
        3,
        jax.ShapeDtypeStruct((4, probes), F32),
        [pltpu.VMEM((4 * LANES, count * blocks), BF16)],
    )(returned, row, lane)


def solution(mesh):
    sizes = tuple(mesh.shape[axis] for axis in AXES)
    placed = (P(AXES, None), P(None, AXES), P(AXES, None), P(AXES))
    return jax.shard_map(
        functools.partial(local, sizes),
        mesh=mesh,
        in_specs=placed,
        out_specs=P(None, AXES),
        check_vma=False,
    )
```

profile of v0, /device:TPU:0, one launch (start us, length us, event | category | flops | bytes accessed | tf_op | source)
XLA Modules:
  0.0 53.8 jit_solution(10963209145285928898)
XLA Ops:
  0.0 1.3 %copy.8 = bf16[128,2048]{0,1:T(8,128)(2,1)S(1)} copy(bf16[128,2048]{1,0:T(8,128)(2,1)} %param.6) | data formatting | bytes 1048576 | tf_op args[0]
  1.3 0.0 copy-start
  1.3 0.0 copy-start.1
  1.3 0.0 copy-start.2
  1.4 0.0 copy-start.3
  1.4 0.1 copy.11
  1.5 0.0 copy-start.4
  1.5 0.7 %copy-done.4 = f32[64]{0:T(128)S(1)} copy-done((f32[64]{0:T(128)S(1)}, f32[64]{0:T(128)}, u32[]{:S(2)}) %copy-start.4) | copy-done | bytes 280
  2.2 0.1 broadcast_in_dim.8.nodes_ref
  2.2 0.0 copy-done
  2.3 0.1 copy-done.1
  2.4 0.0 copy-done.2
  2.4 0.0 copy-done.3
  2.4 43.5 %shard_map.64 = (f32[20,32,128]{2,1,0:T(8,128)S(1)}, f32[1,16384]{1,0:T(1,128)S(1)}, f32[1,16384]{1,0:T(1,128)S(1)}) custom-call(s32[1,16384]{1,0:T(1,128)S(1)} %bitcast.10, f32[3,16384]{1,0:T(4,128)S(1)} %copy-done, s32[1,16384]{1,0:T(1,128)S(1)} %bitcast.11, bf16[256,512]{1,0:T(8,128)(2,1)S(1)} %copy-done.1, bf16[256,1024]{1,0:T(8,128)(2,1)S(1)} %bitcast.9, ...), custom_call_target="tpu_custom_call" | custom-call | tf_op jit(solution)/shard_map/pallas_call | solution.py:340
  45.9 7.9 %shard_map.65 = f32[4,16384]{1,0:T(4,128)} custom-call(f32[20,32,128]{2,1,0:T(8,128)S(1)} %get-tuple-element.8.values_ref, f32[1,16384]{1,0:T(1,128)S(1)} %get-tuple-element.9.row_ref, f32[1,16384]{1,0:T(1,128)S(1)} %get-tuple-element.10.lane_ref), custom_call_target="tpu_custom_call" | custom-call | tf_op jit(solution)/shard_map/pallas_call | solution.py:359
Async XLA Ops:
  1.3 1.0 %copy-start = (f32[3,16384]{1,0:T(4,128)S(1)}, f32[3,16384]{1,0:T(4,128)}, u32[]{:S(2)}) copy-start(f32[3,16384]{1,0:T(4,128)} %coords_ref.1) | copy-start | bytes 589828
  1.3 1.0 %copy-start.1 = (bf16[256,512]{1,0:T(8,128)(2,1)S(1)}, bf16[256,512]{1,0:T(8,128)(2,1)}, u32[]{:S(2)}) copy-start(bf16[256,512]{1,0:T(8,128)(2,1)} %constant.5.clone.prefix_ref) | copy-start | bytes 786436
  1.3 1.0 %copy-start.2 = (s32[16384,1]{0,1:T(1,128)S(1)}, s32[16384,1]{0,1:T(1,128)}, u32[]{:S(2)}) copy-start(s32[16384,1]{0,1:T(1,128)} %param.8) | copy-start | bytes 196612
  1.4 1.0 %copy-start.3 = (s32[16384]{0:T(1024)S(1)}, s32[16384]{0:T(1024)}, u32[]{:S(2)}) copy-start(s32[16384]{0:T(1024)} %param.9) | copy-start | bytes 196612
  1.5 0.7 %copy-start.4 = (f32[64]{0:T(128)S(1)}, f32[64]{0:T(128)}, u32[]{:S(2)}) copy-start(f32[64]{0:T(128)} %constant.6) | copy-start | bytes 772
where the time goes:
time: 53.9 us; the launch traced here: 53.8 us
  Pallas kernels  51.4 us (95%)
  local copies, waits for them, and re-layouts  2.3 us (4%)
    pallas_call x1, Pallas kernels, local(): call(functools.partial(sample_kernel, sizes, blocks), 6, (layout, line, l...  43.5 us
    pallas_call x1, Pallas kernels, local(): call(functools.partial(return_kernel, blocks), 3, jax.ShapeDtypeStruct((4...  7.88 us
    unnamed x12, local copies, waits for them, and re-layouts  2.23 us

commit v1 on v0

v1 whole, which is shorter than its diff:
```python
import functools

import jax
import jax.numpy as jnp
import numpy as np
from jax import lax
from jax.experimental import pallas as pl
from jax.experimental.pallas import tpu as pltpu
from jax.sharding import PartitionSpec as P

AXES = ("gx", "gy", "gz")
F32, BF16 = jnp.float32, jnp.bfloat16
LANES = 128
CHUNK = 256
GROUP = 4
BATCH = 16
SWEEP = 16
STRIDE = 4

gll_points = np.array(
    [
        -1.0,
        -0.8717401485096066,
        -0.5917001814331423,
        -0.2092992179024789,
        0.2092992179024789,
        0.5917001814331423,
        0.8717401485096066,
        1.0,
    ]
)
gll_scale = np.array(
    [1.0 / np.prod([gll_points[a] - gll_points[b] for b in range(8) if b != a]) for a in range(8)]
)


def column(values):
    node = lax.broadcasted_iota(jnp.int32, (8, LANES), 0)
    out = jnp.full((8, LANES), float(values[0]), F32)
    for a in range(1, 8):
        out = jnp.where(node == a, float(values[a]), out)
    return out


def iota_bf16(shape):
    return lax.broadcasted_iota(jnp.int32, shape, 0).astype(F32).astype(BF16)


def spread(row, count):
    return jnp.broadcast_to(row, (count, row.shape[1])).astype(BF16)


def splits(count):
    groups = max(1, 2 * LANES // count)
    return groups, LANES // groups, max(1, LANES // count)


def exchange(pieces, count):
    block = lax.broadcasted_iota(jnp.int32, pieces[0].shape, 1) // count
    bit = len(pieces) // 2
    while bit:
        high = (block // bit) % 2 == 1
        swapped = []
        for i, own in enumerate(pieces):
            upper = (i // bit) % 2 == 1
            other = pltpu.roll(pieces[i - bit if upper else i + bit], LANES - bit * count if upper else bit * count, 1)
            swapped.append(jnp.where(high, own, other) if upper else jnp.where(high, other, own))
        pieces = swapped
        bit //= 2
    return pieces


def prepare(prefix_ref, nodes_ref):
    below = lax.broadcasted_iota(jnp.int32, (CHUNK, CHUNK), 0) <= lax.broadcasted_iota(jnp.int32, (CHUNK, CHUNK), 1)
    prefix_ref[:, :CHUNK] = jnp.where(below, 1.0, 0.0).astype(BF16)
    prefix_ref[:, CHUNK:] = jnp.ones((CHUNK, CHUNK), BF16)
    nodes_ref[0:8, :] = column(gll_scale)
    for k in range(1, 8):
        nodes_ref[8 * k : 8 * k + 8, :] = column(np.roll(gll_points, -k))


def turn(tile, fields_ref, turned_ref, flip_ref):
    elements = fields_ref.shape[0]
    columns = pl.ds(pl.multiple_of(tile * LANES, LANES), LANES)
    rows = pl.ds(pl.multiple_of(tile * 16, 16), 16)
    flip_ref[...] = fields_ref[:, columns].astype(F32).T
    near, nodes = elements // 2, turned_ref.shape[0] // 2
    beyond = pl.ds(pl.multiple_of(nodes + tile * 16, 16), 16)
    for c in range(0, 8, 2):
        one, two = [flip_ref[pl.ds(c + i, 16, stride=8), :] for i in range(2)]
        left = lax.broadcasted_iota(jnp.int32, one.shape, 1) < near
        turned_ref[rows, c * near : (c + 2) * near] = jnp.where(left, one, pltpu.roll(two, near, 1)).astype(BF16)
        turned_ref[beyond, c * near : (c + 2) * near] = jnp.where(left, pltpu.roll(one, near, 1), two).astype(BF16)


def place_all(count, rank_ref, prefix_ref, row_ref, lane_ref):
    probes = rank_ref.shape[1]
    group = max(1, CHUNK // count)
    groups, width, _ = splits(count)
    targets = lax.broadcasted_iota(jnp.int32, (count, CHUNK), 0)

    def place(outer, carry):
        for inner in range(STRIDE):
            step = outer * STRIDE + inner
            masks, hots, ranks = [], [], []
            for g in range(group):
                at = pl.ds(pl.multiple_of((step * group + g) * CHUNK, CHUNK), CHUNK)
                rank = rank_ref[:, at]
                mask = targets == jnp.broadcast_to(rank, (count, CHUNK))
                masks.append(mask)
                hots.append(jnp.where(mask, 1.0, 0.0).astype(BF16))
                ranks.append(rank.astype(F32))
            counted = jnp.dot(jnp.concatenate(hots, axis=0), prefix_ref[...], preferred_element_type=F32)
            for g in range(group):
                at = pl.ds(pl.multiple_of((step * group + g) * CHUNK, CHUNK), CHUNK)
                piece = counted[g * count : (g + 1) * count]
                place_in = jnp.where(masks[g], piece[:, :CHUNK] + carry, 0.0)
                position = jnp.sum(place_in, axis=0, keepdims=True) - 1.0
                part = jnp.floor(position * (1.0 / width))
                block = jnp.floor(part * (1.0 / groups))
                lane_ref[:, at] = position - (part - block) * width
                row_ref[:, at] = (part - block * groups) * count + ranks[g]
                carry = carry + piece[:, CHUNK:]
        return carry

    lax.fori_loop(0, probes // (CHUNK * group * STRIDE), place, jnp.zeros((count, CHUNK), F32))


def route(count, blocks, coords_ref, slot_ref, fields_ref, turned_ref, flip_ref, send_ref, row_ref, lane_ref, acc_ref):
    probes = slot_ref.shape[1]
    groups, width, per = splits(count)
    rows = groups * count
    spots = blocks * width
    tiles = fields_ref.shape[1] // LANES
    steps = probes // (BATCH * CHUNK)
    row_ids = iota_bf16((rows, CHUNK))
    lane_ids = iota_bf16((spots, CHUNK))
    one, zero = jnp.ones((), BF16), jnp.zeros((), BF16)
    acc_ref[...] = jnp.zeros_like(acc_ref)

    def scatter(step, _):
        row_hots, lane_parts = [], []
        for g in range(BATCH):
            at = pl.ds(pl.multiple_of((step * BATCH + g) * CHUNK, CHUNK), CHUNK)
            row_hots.append(jnp.where(row_ids == spread(row_ref[:, at], rows), one, zero))
            here = lane_ids == spread(lane_ref[:, at], spots)
            parts = []
            for v in range(3):
                value = coords_ref[v : v + 1, at]
                high = value.astype(BF16).astype(F32)
                parts += [high, value - high]
            parts.append(slot_ref[:, at].astype(F32))
            lane_parts.append(jnp.concatenate([jnp.where(here, spread(part, spots), zero) for part in parts], axis=0))
        acc_ref[...] += lax.dot_general(
            jnp.concatenate(lane_parts, axis=1),
            jnp.concatenate(row_hots, axis=1),
            (((1,), (1,)), ((), ())),
            preferred_element_type=F32,
        )
        for tile in range(tiles // steps):
            turn(step * (tiles // steps) + tile, fields_ref, turned_ref, flip_ref)
        return 0

    lax.fori_loop(0, steps, scatter, 0)
    for b in range(blocks):
        for first in range(0, 4, per):
            stacked = []
            for half in range(groups // per):
                columns = slice(half * LANES, (half + 1) * LANES)
                pieces = []
                for v in range(first, first + per):
                    at = 2 * v * spots + b * width
                    piece = acc_ref[at : at + width, columns]
                    if v < 3:
                        piece = piece + acc_ref[at + spots : at + spots + width, columns]
                    pieces.append(piece)
                stacked += exchange(pieces, count)
            flipped = jnp.concatenate(stacked, axis=0).T
            for v in range(first, first + per):
                send_ref[v * blocks + b] = flipped[(v - first) * count : (v - first + 1) * count]


def lagrange(coord, nodes_ref):
    weight = nodes_ref[0:8, :]
    spread_coord = jnp.broadcast_to(coord, (8, LANES))
    for k in range(1, 8):
        weight = weight * (spread_coord - nodes_ref[8 * k : 8 * k + 8, :])
    return weight


def interpolate(blocks, block, sources, recv_ref, fields_ref, nodes_ref, values_ref, picker_ref):
    near = fields_ref.shape[1] // 8
    nodes = fields_ref.shape[0] // 2
    zero = jnp.zeros((), BF16)
    ids = iota_bf16((near, LANES))
    weights = []
    for j, source in enumerate(sources):
        r, s, t, slot = [recv_ref[v * blocks + block, pl.ds(source, 1), :] for v in range(4)]
        weight_t = lagrange(t, nodes_ref)
        columns = slice(j * LANES, (j + 1) * LANES)
        far = jnp.broadcast_to(slot, (8, LANES)) >= float(near)
        mask = ids == spread(jnp.where(far[0:1], slot - float(near), slot), near)
        for c in range(8):
            picker_ref[c * near : (c + 1) * near, columns] = jnp.where(mask, spread(weight_t[c : c + 1, :], near), zero)
        weights.append((lagrange(r, nodes_ref), lagrange(s, nodes_ref), far))
    along = jnp.dot(fields_ref[...], picker_ref[...], preferred_element_type=F32)
    for j, source in enumerate(sources):
        weight_r, weight_s, far = weights[j]
        columns = slice(j * LANES, (j + 1) * LANES)
        factors = [jnp.broadcast_to(weight_r[a : a + 1, :], (8, LANES)) for a in range(8)]
        for f in range(4):
            total = None
            for a in range(8):
                at = f * 64 + a * 8
                here = jnp.where(far, along[nodes + at : nodes + at + 8, columns], along[at : at + 8, columns])
                total = here * factors[a] if a == 0 else total + here * factors[a]
            values_ref[f * blocks + block, pl.ds(source, 1), :] = jnp.sum(
                total * weight_s, axis=0, keepdims=True
            )


def sample_kernel(
    sizes,
    blocks,
    rank_in,
    coords_in,
    slot_in,
    fields_in,
    back_ref,
    row_ref,
    lane_ref,
    rank_ref,
    coords_ref,
    slot_ref,
    fields_ref,
    prefix_ref,
    nodes_ref,
    turned_ref,
    flip_ref,
    acc_ref,
    send_ref,
    recv_ref,
    values_ref,
    picker_even,
    picker_odd,
    out_sem,
    in_sem,
    back_out_sem,
    back_in_sem,
    own_sem,
    load_sem,
):
    count = sizes[0] * sizes[1] * sizes[2]
    place = [lax.axis_index(axis) for axis in AXES]
    me = (place[0] * sizes[1] + place[1]) * sizes[2] + place[2]
    mesh_ids = pl.DeviceIdType.MESH

    def peer(step, sign):
        offsets = [step // (sizes[1] * sizes[2]), step // sizes[2] % sizes[1], step % sizes[2]]
        at = tuple(lax.rem(p + n + sign * o, n) for p, n, o in zip(place, sizes, offsets))
        return (at[0] * sizes[1] + at[1]) * sizes[2] + at[2], at

    def each(first, last, act):
        def body(step, _):
            act(step)
            return 0

        lax.fori_loop(first, last, body, 0)

    def outward(step):
        other, at = peer(step, 1)
        return pltpu.make_async_remote_copy(
            src_ref=send_ref.at[:, other],
            dst_ref=recv_ref.at[:, me],
            send_sem=out_sem.at[step],
            recv_sem=in_sem.at[step],
            device_id=at,
            device_id_type=mesh_ids,
        )

    def backward(step):
        other, at = peer(step, -1)
        return pltpu.make_async_remote_copy(
            src_ref=values_ref.at[:, other],
            dst_ref=back_ref.at[:, me],
            send_sem=back_out_sem.at[step],
            recv_sem=back_in_sem.at[step],
            device_id=at,
            device_id_type=mesh_ids,
        )

    loads = [
        pltpu.make_async_copy(source, target, load_sem.at[i])
        for i, (source, target) in enumerate(
            [(rank_in, rank_ref), (coords_in, coords_ref), (slot_in, slot_ref), (fields_in, fields_ref)]
        )
    ]
    for load in loads:
        load.start()
    barrier = pltpu.get_barrier_semaphore()
    for step in range(1, count):
        pl.semaphore_signal(barrier, inc=1, device_id=peer(step, 1)[1], device_id_type=mesh_ids)
    prepare(prefix_ref, nodes_ref)
    loads[0].wait()
    place_all(count, rank_ref, prefix_ref, row_ref, lane_ref)
    for load in loads[1:]:
        load.wait()
    route(count, blocks, coords_ref, slot_ref, fields_ref, turned_ref, flip_ref, send_ref, row_ref, lane_ref, acc_ref)
    pl.semaphore_wait(barrier, count - 1)
    for step in range(1, count):
        outward(step).start()
    own = pltpu.make_async_copy(send_ref.at[:, me], recv_ref.at[:, me], own_sem.at[0])
    own.start()
    own.wait()
    own_back = pltpu.make_async_copy(values_ref.at[:, me], back_ref.at[:, me], own_sem.at[1])
    pickers = [picker_even, picker_odd]

    def reply(group):
        for j in range(GROUP):
            step = group * GROUP + j
            if j == 0:

                @pl.when(step == 0)
                def _():
                    own_back.start()

                @pl.when(step > 0)
                def _():
                    backward(step).start()

            else:
                backward(step).start()

    def body(group, _):
        @pl.when(group > 0)
        def _():
            reply(group - 1)

        sources = []
        for j in range(GROUP):
            step = group * GROUP + j
            if j == 0:

                @pl.when(step > 0)
                def _():
                    outward(step).wait_recv()

            else:
                outward(step).wait_recv()
            sources.append(peer(step, -1)[0])
        for block in range(blocks):
            interpolate(blocks, block, sources, recv_ref, turned_ref, nodes_ref, values_ref, pickers[block % 2])
        return 0

    groups = count // GROUP
    lax.fori_loop(0, groups, body, 0)
    reply(groups - 1)
    each(1, count, lambda step: outward(step).wait_send())
    each(1, count, lambda step: backward(step).wait())
    own_back.wait()


def return_kernel(blocks, values_ref, row_ref, lane_ref, out_ref, table_ref):
    probes = row_ref.shape[1]
    count = values_ref.shape[1]
    groups, width, per = splits(count)
    rows = groups * count
    spots = blocks * width
    for b in range(blocks):
        for first in range(0, 4, per):
            stacked = [values_ref[f * blocks + b] for f in range(first, first + per)]
            flipped = jnp.concatenate(stacked, axis=0).T
            for half in range(groups // per):
                pieces = [flipped[(half * per + q) * width : (half * per + q + 1) * width] for q in range(per)]
                for f, piece in enumerate(exchange(pieces, count), first):
                    at = f * spots + b * width
                    table_ref[at : at + width, half * LANES : (half + 1) * LANES] = piece.astype(BF16)
    row_ids = iota_bf16((rows, CHUNK))
    lane_ids = lax.broadcasted_iota(jnp.int32, (spots, CHUNK), 0).astype(F32)

    def body(step, _):
        for g in range(SWEEP):
            at = pl.ds(pl.multiple_of((step * SWEEP + g) * CHUNK, CHUNK), CHUNK)
            hot = jnp.where(row_ids == spread(row_ref[:, at], rows), jnp.ones((), BF16), jnp.zeros((), BF16))
            picked = jnp.dot(table_ref[...], hot, preferred_element_type=F32)
            here = lane_ids == jnp.broadcast_to(lane_ref[:, at], (spots, CHUNK))
            for f in range(4):
                out_ref[f : f + 1, at] = jnp.sum(
                    jnp.where(here, picked[f * spots : (f + 1) * spots], 0.0), axis=0, keepdims=True
                )
        return 0

    lax.fori_loop(0, probes // (SWEEP * CHUNK), body, 0)


VMEM = pl.BlockSpec(memory_space=pltpu.VMEM)
HBM = pl.BlockSpec(memory_space=pltpu.HBM)


def call(kernel, inputs, outputs, scratch, **options):
    return pl.pallas_call(
        kernel,
        out_shape=outputs,
        in_specs=inputs,
        out_specs=jax.tree.map(lambda _: VMEM, outputs),
        scratch_shapes=scratch,
        compiler_params=pltpu.CompilerParams(vmem_limit_bytes=48 << 20, **options),
    )


def local(sizes, fields, coordinates, element_rank, element_slot):
    count = sizes[0] * sizes[1] * sizes[2]
    probes = element_slot.shape[0]
    elements = fields.shape[0]
    capacity = 5 * probes // (4 * count)
    blocks = -(-capacity // LANES)
    layout = jax.ShapeDtypeStruct((4 * blocks, count, LANES), F32)
    line = jax.ShapeDtypeStruct((1, probes), F32)

    groups, width, _ = splits(count)
    spots, rows = blocks * width, groups * count
    depth = fields.shape[1] // 8
    picker = pltpu.VMEM((4 * elements, GROUP * LANES), BF16)
    buffer = pltpu.VMEM(layout.shape, F32)
    arrivals = pltpu.SemaphoreType.DMA((count,))
    returned, row, lane = call(
        functools.partial(sample_kernel, sizes, blocks),
        [HBM] * 4,
        (layout, line, line),
        [
            pltpu.VMEM((1, probes), jnp.int32),
            pltpu.VMEM((3, probes), F32),
            pltpu.VMEM((1, probes), jnp.int32),
            pltpu.VMEM(fields.shape, BF16),
            pltpu.VMEM((CHUNK, 2 * CHUNK), BF16),
            pltpu.VMEM((64, LANES), F32),
            pltpu.VMEM((2 * depth, 4 * elements), BF16),
            pltpu.VMEM((LANES, elements), F32),
            pltpu.VMEM((7 * spots, rows), F32),
        ]
        + [buffer] * 3
        + [picker] * 2
        + [arrivals] * 4
        + [pltpu.SemaphoreType.DMA((2,)), pltpu.SemaphoreType.DMA((4,))],
        collective_id=0,
        has_side_effects=True,
    )(
        *[
            pltpu.with_memory_space_constraint(x, pltpu.HBM)
            for x in (element_rank.reshape(1, probes), coordinates, element_slot.reshape(1, probes), fields)
        ]
    )
    return call(
        functools.partial(return_kernel, blocks),
        [VMEM] * 3,
        jax.ShapeDtypeStruct((4, probes), F32),
        [pltpu.VMEM((4 * spots, rows), BF16)],
    )(returned, row, lane)


def solution(mesh):
    sizes = tuple(mesh.shape[axis] for axis in AXES)
    placed = (P(AXES, None), P(None, AXES), P(AXES, None), P(AXES))
    return jax.shard_map(
        functools.partial(local, sizes),
        mesh=mesh,
        in_specs=placed,
        out_specs=P(None, AXES),
        check_vma=False,
    )
```

time: 53.9 us -> 41.5 us (0.77)
  Pallas kernels: 51.4 us -> 41.3 us
  local copies, waits for them, and re-layouts: 2.3 us -> 0 us
    pallas_call x2, Pallas kernels: 51.4 us -> 41.3 us  [the longest x1 36.7 us: local(): call(functools.partial(sample_kernel, sizes, blocks), [HBM] * 4, (layout,...]
    unnamed x12 -> x0, local copies, waits for them, and re-layouts: 2.23 us -> none
where the time goes in v1:
time: 41.5 us; the launch traced here: 41.3 us
  Pallas kernels  41.3 us (100%)
    pallas_call x1, Pallas kernels, local(): call(functools.partial(sample_kernel, sizes, blocks), [HBM] * 4, (layout,...  36.7 us
    pallas_call x1, Pallas kernels, local(): call(functools.partial(return_kernel, blocks), [VMEM] * 3, jax.ShapeDtype...  4.63 us

profile of v1, /device:TPU:0, one launch (start us, length us, event | category | flops | bytes accessed | tf_op | source)
XLA Modules:
  0.0 41.3 jit_solution(4524750509599111173)
XLA Ops:
  0.0 36.7 %shard_map.46 = (f32[20,32,128]{2,1,0:T(8,128)S(1)}, f32[1,16384]{1,0:T(1,128)S(1)}, f32[1,16384]{1,0:T(1,128)S(1)}) custom-call(s32[1,16384]{1,0:T(1,128)} %bitcast.2, f32[3,16384]{1,0:T(4,128)} %coords_in.1, s32[1,16384]{1,0:T(1,128)} %bitcast.3, bf16[128,2048]{1,0:T(8,128)(2,1)} %fields_in.1), custom_call_target="tpu_custom_call" | custom-call | tf_op jit(solution)/shard_map/pallas_call | solution.py:426
  36.7 4.6 %shard_map.47 = f32[4,16384]{1,0:T(4,128)} custom-call(f32[20,32,128]{2,1,0:T(8,128)S(1)} %get-tuple-element.8.values_ref, f32[1,16384]{1,0:T(1,128)S(1)} %get-tuple-element.9.row_ref, f32[1,16384]{1,0:T(1,128)S(1)} %get-tuple-element.10.lane_ref), custom_call_target="tpu_custom_call" | custom-call | tf_op jit(solution)/shard_map/pallas_call | solution.py:453

commit v2 on v1

--- a/solution.py
+++ b/solution.py
@@ -14,8 +14,8 @@
 CHUNK = 256
 GROUP = 4
 BATCH = 16
-SWEEP = 16
-STRIDE = 4
+SWEEP = 32
+SPAN = 1024.0
 
 gll_points = np.array(
     [
@@ -93,52 +93,89 @@
         turned_ref[beyond, c * near : (c + 2) * near] = jnp.where(left, pltpu.roll(one, near, 1), two).astype(BF16)
 
 
-def place_all(count, rank_ref, prefix_ref, row_ref, lane_ref):
-    probes = rank_ref.shape[1]
-    group = max(1, CHUNK // count)
+def offset_bits(sizes, group, j):
+    rest = sizes[0] * sizes[1] * sizes[2] // (2 * GROUP)
+    if isinstance(group, int):
+        hot = int(1 <= group <= rest)
+        which = group - 1 if hot else max(group - rest, 0)
+    else:
+        hot = (group + rest - 1) // rest % 2
+        which = hot * (group - 1) + (1 - hot) * jnp.maximum(group - rest, 0)
+    width = sum((n - 1).bit_length() for n in sizes)
+    return [j % 2, j // 2 % 2, hot] + [which // 2**k % 2 for k in range(width - 3)]
+
+
+def peer_of(sizes, place, group, j):
+    bits = offset_bits(sizes, group, j)
+    at = list(place)
+    for axis in (2, 1, 0):
+        for k in range((sizes[axis] - 1).bit_length()):
+            at[axis] = at[axis] + bits.pop(0) * (1 - place[axis] // 2**k % 2 * 2) * 2**k
+    return tuple(at)
+
+
+def place_batch(count, step, targets, carry, rank_ref, prefix_ref, row_ref, lane_ref):
+    group = min(BATCH, max(1, CHUNK // count))
     groups, width, _ = splits(count)
-    targets = lax.broadcasted_iota(jnp.int32, (count, CHUNK), 0)
-
-    def place(outer, carry):
-        for inner in range(STRIDE):
-            step = outer * STRIDE + inner
-            masks, hots, ranks = [], [], []
-            for g in range(group):
-                at = pl.ds(pl.multiple_of((step * group + g) * CHUNK, CHUNK), CHUNK)
-                rank = rank_ref[:, at]
-                mask = targets == jnp.broadcast_to(rank, (count, CHUNK))
-                masks.append(mask)
-                hots.append(jnp.where(mask, 1.0, 0.0).astype(BF16))
-                ranks.append(rank.astype(F32))
-            counted = jnp.dot(jnp.concatenate(hots, axis=0), prefix_ref[...], preferred_element_type=F32)
-            for g in range(group):
-                at = pl.ds(pl.multiple_of((step * group + g) * CHUNK, CHUNK), CHUNK)
-                piece = counted[g * count : (g + 1) * count]
-                place_in = jnp.where(masks[g], piece[:, :CHUNK] + carry, 0.0)
-                position = jnp.sum(place_in, axis=0, keepdims=True) - 1.0
-                part = jnp.floor(position * (1.0 / width))
-                block = jnp.floor(part * (1.0 / groups))
-                lane_ref[:, at] = position - (part - block) * width
-                row_ref[:, at] = (part - block * groups) * count + ranks[g]
-                carry = carry + piece[:, CHUNK:]
-        return carry
-
-    lax.fori_loop(0, probes // (CHUNK * group * STRIDE), place, jnp.zeros((count, CHUNK), F32))
-
-
-def route(count, blocks, coords_ref, slot_ref, fields_ref, turned_ref, flip_ref, send_ref, row_ref, lane_ref, acc_ref):
+    for inner in range(BATCH // group):
+        masks, hots = [], []
+        places = [
+            pl.ds(pl.multiple_of((step * BATCH + inner * group + g) * CHUNK, CHUNK), CHUNK) for g in range(group)
+        ]
+        for at in places:
+            mask = targets == jnp.broadcast_to(rank_ref[:, at], (count, CHUNK))
+            masks.append(mask)
+            hots.append(jnp.where(mask, 1.0, 0.0).astype(BF16))
+        counted = jnp.dot(jnp.concatenate(hots, axis=0), prefix_ref[...], preferred_element_type=F32)
+        for g, at in enumerate(places):
+            piece = counted[g * count : (g + 1) * count]
+            place_in = jnp.where(masks[g], piece[:, :CHUNK] + carry, 0.0)
+            found = jnp.sum(place_in, axis=0, keepdims=True) - 1.0
+            peer = jnp.floor(found * (1.0 / SPAN))
+            position = found - peer * SPAN
+            part = jnp.floor(position * (1.0 / width))
+            block = jnp.floor(part * (1.0 / groups))
+            lane_ref[:, at] = position - (part - block) * width
+            row_ref[:, at] = (part - block * groups) * count + peer
+            carry = carry + piece[:, CHUNK:]
+    return carry
+
+
+def route(
+    sizes,
+    place,
+    blocks,
+    loads,
+    rank_ref,
+    coords_ref,
+    slot_ref,
+    fields_ref,
+    prefix_ref,
+    turned_ref,
+    flip_ref,
+    row_ref,
+    lane_ref,
+    acc_ref,
+):
+    count = sizes[0] * sizes[1] * sizes[2]
     probes = slot_ref.shape[1]
     groups, width, per = splits(count)
     rows = groups * count
     spots = blocks * width
     tiles = fields_ref.shape[1] // LANES
     steps = probes // (BATCH * CHUNK)
+    steps_of = lax.broadcasted_iota(jnp.int32, (count, CHUNK), 0)
+    x, y, z = peer_of(sizes, place, steps_of // GROUP, steps_of % GROUP)
+    targets = (x * sizes[1] + y) * sizes[2] + z
     row_ids = iota_bf16((rows, CHUNK))
     lane_ids = iota_bf16((spots, CHUNK))
     one, zero = jnp.ones((), BF16), jnp.zeros((), BF16)
     acc_ref[...] = jnp.zeros_like(acc_ref)
 
-    def scatter(step, _):
+    def put(step, carry):
+        return place_batch(count, step, targets, carry, rank_ref, prefix_ref, row_ref, lane_ref)
+
+    def scatter(step):
         row_hots, lane_parts = [], []
         for g in range(BATCH):
             at = pl.ds(pl.multiple_of((step * BATCH + g) * CHUNK, CHUNK), CHUNK)
@@ -159,9 +196,22 @@
         )
         for tile in range(tiles // steps):
             turn(step * (tiles // steps) + tile, fields_ref, turned_ref, flip_ref)
-        return 0
-
-    lax.fori_loop(0, steps, scatter, 0)
+
+    def both(step, carry):
+        scatter(step)
+        return put(step + 1, carry)
+
+    rank_ref[:, probes:] = jnp.zeros((1, rank_ref.shape[1] - probes), jnp.int32)
+    loads[0].wait()
+    carry = put(0, steps_of.astype(F32) * SPAN)
+    for load in loads[1:]:
+        load.wait()
+    lax.fori_loop(0, steps, both, carry)
+
+
+def assemble(count, blocks, acc_ref, send_ref, recv_ref):
+    groups, width, per = splits(count)
+    spots = blocks * width
     for b in range(blocks):
         for first in range(0, 4, per):
             stacked = []
@@ -178,6 +228,7 @@
             flipped = jnp.concatenate(stacked, axis=0).T
             for v in range(first, first + per):
                 send_ref[v * blocks + b] = flipped[(v - first) * count : (v - first + 1) * count]
+                recv_ref[v * blocks + b, 0:1] = flipped[(v - first) * count : (v - first) * count + 1]
 
 
 def lagrange(coord, nodes_ref):
@@ -188,24 +239,27 @@
     return weight
 
 
-def interpolate(blocks, block, sources, recv_ref, fields_ref, nodes_ref, values_ref, picker_ref):
-    near = fields_ref.shape[1] // 8
-    nodes = fields_ref.shape[0] // 2
+def pick(blocks, block, first, recv_ref, nodes_ref, picker_ref):
+    near = picker_ref.shape[0] // 8
     zero = jnp.zeros((), BF16)
     ids = iota_bf16((near, LANES))
-    weights = []
-    for j, source in enumerate(sources):
-        r, s, t, slot = [recv_ref[v * blocks + block, pl.ds(source, 1), :] for v in range(4)]
+    for j in range(GROUP):
+        t, slot = [recv_ref[v * blocks + block, pl.ds(first + j, 1), :] for v in (2, 3)]
         weight_t = lagrange(t, nodes_ref)
         columns = slice(j * LANES, (j + 1) * LANES)
-        far = jnp.broadcast_to(slot, (8, LANES)) >= float(near)
-        mask = ids == spread(jnp.where(far[0:1], slot - float(near), slot), near)
+        mask = ids == spread(jnp.where(slot >= float(near), slot - float(near), slot), near)
         for c in range(8):
             picker_ref[c * near : (c + 1) * near, columns] = jnp.where(mask, spread(weight_t[c : c + 1, :], near), zero)
-        weights.append((lagrange(r, nodes_ref), lagrange(s, nodes_ref), far))
+
+
+def combine(blocks, block, first, recv_ref, fields_ref, nodes_ref, values_ref, picker_ref):
+    near = picker_ref.shape[0] // 8
+    nodes = fields_ref.shape[0] // 2
     along = jnp.dot(fields_ref[...], picker_ref[...], preferred_element_type=F32)
-    for j, source in enumerate(sources):
-        weight_r, weight_s, far = weights[j]
+    for j in range(GROUP):
+        r, s, slot = [recv_ref[v * blocks + block, pl.ds(first + j, 1), :] for v in (0, 1, 3)]
+        weight_r, weight_s = lagrange(r, nodes_ref), lagrange(s, nodes_ref)
+        far = jnp.broadcast_to(slot, (8, LANES)) >= float(near)
         columns = slice(j * LANES, (j + 1) * LANES)
         factors = [jnp.broadcast_to(weight_r[a : a + 1, :], (8, LANES)) for a in range(8)]
         for f in range(4):
@@ -214,7 +268,7 @@
                 at = f * 64 + a * 8
                 here = jnp.where(far, along[nodes + at : nodes + at + 8, columns], along[at : at + 8, columns])
                 total = here * factors[a] if a == 0 else total + here * factors[a]
-            values_ref[f * blocks + block, pl.ds(source, 1), :] = jnp.sum(
+            values_ref[f * blocks + block, pl.ds(first + j, 1), :] = jnp.sum(
                 total * weight_s, axis=0, keepdims=True
             )
 
@@ -247,18 +301,11 @@
     in_sem,
     back_out_sem,
     back_in_sem,
-    own_sem,
     load_sem,
 ):
     count = sizes[0] * sizes[1] * sizes[2]
     place = [lax.axis_index(axis) for axis in AXES]
-    me = (place[0] * sizes[1] + place[1]) * sizes[2] + place[2]
     mesh_ids = pl.DeviceIdType.MESH
-
-    def peer(step, sign):
-        offsets = [step // (sizes[1] * sizes[2]), step // sizes[2] % sizes[1], step % sizes[2]]
-        at = tuple(lax.rem(p + n + sign * o, n) for p, n, o in zip(place, sizes, offsets))
-        return (at[0] * sizes[1] + at[1]) * sizes[2] + at[2], at
 
     def each(first, last, act):
         def body(step, _):
@@ -267,101 +314,108 @@
 
         lax.fori_loop(first, last, body, 0)
 
-    def outward(step):
-        other, at = peer(step, 1)
+    def outward(group, j):
+        step = group * GROUP + j
         return pltpu.make_async_remote_copy(
-            src_ref=send_ref.at[:, other],
-            dst_ref=recv_ref.at[:, me],
+            src_ref=send_ref.at[:, step],
+            dst_ref=recv_ref.at[:, step],
             send_sem=out_sem.at[step],
             recv_sem=in_sem.at[step],
-            device_id=at,
+            device_id=peer_of(sizes, place, group, j),
             device_id_type=mesh_ids,
         )
 
-    def backward(step):
-        other, at = peer(step, -1)
+    def backward(group, j):
+        step = group * GROUP + j
         return pltpu.make_async_remote_copy(
-            src_ref=values_ref.at[:, other],
-            dst_ref=back_ref.at[:, me],
+            src_ref=values_ref.at[:, step],
+            dst_ref=back_ref.at[:, step],
             send_sem=back_out_sem.at[step],
             recv_sem=back_in_sem.at[step],
-            device_id=at,
+            device_id=peer_of(sizes, place, group, j),
             device_id_type=mesh_ids,
         )
 
     loads = [
         pltpu.make_async_copy(source, target, load_sem.at[i])
         for i, (source, target) in enumerate(
-            [(rank_in, rank_ref), (coords_in, coords_ref), (slot_in, slot_ref), (fields_in, fields_ref)]
+            [(rank_in, rank_ref.at[:, : rank_in.shape[1]]), (coords_in, coords_ref), (slot_in, slot_ref), (fields_in, fields_ref)]
         )
     ]
     for load in loads:
         load.start()
     barrier = pltpu.get_barrier_semaphore()
-    for step in range(1, count):
-        pl.semaphore_signal(barrier, inc=1, device_id=peer(step, 1)[1], device_id_type=mesh_ids)
+    others = [(group, j) for group in range(count // GROUP) for j in range(GROUP) if group or j]
+    for group, j in others:
+        pl.semaphore_signal(barrier, inc=1, device_id=peer_of(sizes, place, group, j), device_id_type=mesh_ids)
     prepare(prefix_ref, nodes_ref)
-    loads[0].wait()
-    place_all(count, rank_ref, prefix_ref, row_ref, lane_ref)
-    for load in loads[1:]:
-        load.wait()
-    route(count, blocks, coords_ref, slot_ref, fields_ref, turned_ref, flip_ref, send_ref, row_ref, lane_ref, acc_ref)
+    route(
+        sizes,
+        place,
+        blocks,
+        loads,
+        rank_ref,
+        coords_ref,
+        slot_ref,
+        fields_ref,
+        prefix_ref,
+        turned_ref,
+        flip_ref,
+        row_ref,
+        lane_ref,
+        acc_ref,
+    )
     pl.semaphore_wait(barrier, count - 1)
-    for step in range(1, count):
-        outward(step).start()
-    own = pltpu.make_async_copy(send_ref.at[:, me], recv_ref.at[:, me], own_sem.at[0])
-    own.start()
-    own.wait()
-    own_back = pltpu.make_async_copy(values_ref.at[:, me], back_ref.at[:, me], own_sem.at[1])
+    assemble(count, blocks, acc_ref, send_ref, recv_ref)
+    for group, j in others:
+        outward(group, j).start()
+    groups = count // GROUP
     pickers = [picker_even, picker_odd]
 
-    def reply(group):
-        for j in range(GROUP):
-            step = group * GROUP + j
-            if j == 0:
-
-                @pl.when(step == 0)
-                def _():
-                    own_back.start()
-
-                @pl.when(step > 0)
-                def _():
-                    backward(step).start()
-
-            else:
-                backward(step).start()
+    def reply(group, skip):
+        for j in range(skip, GROUP):
+            backward(group, j).start()
+
+    def serve(group):
+        first = group * GROUP
+        for block in range(blocks):
+            pick(blocks, block, first, recv_ref, nodes_ref, pickers[block % 2])
+            combine(blocks, block, first, recv_ref, turned_ref, nodes_ref, values_ref, pickers[block % 2])
 
     def body(group, _):
+        @pl.when(group > 1)
+        def _():
+            backward(group - 1, 0).start()
+
         @pl.when(group > 0)
         def _():
-            reply(group - 1)
-
-        sources = []
-        for j in range(GROUP):
-            step = group * GROUP + j
-            if j == 0:
-
-                @pl.when(step > 0)
-                def _():
-                    outward(step).wait_recv()
-
-            else:
-                outward(step).wait_recv()
-            sources.append(peer(step, -1)[0])
-        for block in range(blocks):
-            interpolate(blocks, block, sources, recv_ref, turned_ref, nodes_ref, values_ref, pickers[block % 2])
+            reply(group - 1, 1)
+            outward(group, 0).wait_recv()
+
+        for j in range(1, GROUP):
+            outward(group, j).wait_recv()
+        serve(group)
         return 0
 
-    groups = count // GROUP
     lax.fori_loop(0, groups, body, 0)
-    reply(groups - 1)
-    each(1, count, lambda step: outward(step).wait_send())
-    each(1, count, lambda step: backward(step).wait())
-    own_back.wait()
+    reply(groups - 1, 0)
+    back_ref[:, 0:1] = values_ref[:, 0:1]
+
+    def finish(group, skip):
+        for j in range(skip, GROUP):
+            outward(group, j).wait_send()
+            backward(group, j).wait()
+
+    def rest(group, _):
+        finish(group, 0)
+        return 0
+
+    finish(0, 1)
+    lax.fori_loop(1, groups, rest, 0)
 
 
 def return_kernel(blocks, values_ref, row_ref, lane_ref, out_ref, table_ref):
-    probes = row_ref.shape[1]
+    probes = out_ref.shape[1]
     count = values_ref.shape[1]
     groups, width, per = splits(count)
     rows = groups * count
@@ -415,7 +469,7 @@
     capacity = 5 * probes // (4 * count)
     blocks = -(-capacity // LANES)
     layout = jax.ShapeDtypeStruct((4 * blocks, count, LANES), F32)
-    line = jax.ShapeDtypeStruct((1, probes), F32)
+    line = jax.ShapeDtypeStruct((1, probes + BATCH * CHUNK), F32)
 
     groups, width, _ = splits(count)
     spots, rows = blocks * width, groups * count
@@ -428,7 +482,7 @@
         [HBM] * 4,
         (layout, line, line),
         [
-            pltpu.VMEM((1, probes), jnp.int32),
+            pltpu.VMEM(line.shape, jnp.int32),
             pltpu.VMEM((3, probes), F32),
             pltpu.VMEM((1, probes), jnp.int32),
             pltpu.VMEM(fields.shape, BF16),
@@ -441,7 +495,7 @@
         + [buffer] * 3
         + [picker] * 2
         + [arrivals] * 4
-        + [pltpu.SemaphoreType.DMA((2,)), pltpu.SemaphoreType.DMA((4,))],
+        + [pltpu.SemaphoreType.DMA((4,))],
         collective_id=0,
         has_side_effects=True,
     )(

time: 41.5 us -> 39.7 us (0.957)
  Pallas kernels: 41.3 us -> 39.6 us
    pallas_call x1, Pallas kernels: 36.7 us -> 35.3 us  [local(): call(functools.partial(sample_kernel, sizes, blocks), [HBM] * 4, (layout,...]
where the time goes in v2:
time: 39.7 us; the launch traced here: 39.6 us
  Pallas kernels  39.6 us (100%)
    pallas_call x1, Pallas kernels, local(): call(functools.partial(sample_kernel, sizes, blocks), [HBM] * 4, (layout,...  35.3 us
    pallas_call x1, Pallas kernels, local(): call(functools.partial(return_kernel, blocks), [VMEM] * 3, jax.ShapeDtype...  4.3 us

profile of v2, /device:TPU:0, one launch (start us, length us, event | category | flops | bytes accessed | tf_op | source)
XLA Modules:
  0.0 39.6 jit_solution(8122826687144479762)
XLA Ops:
  0.0 35.3 %shard_map.46 = (f32[20,32,128]{2,1,0:T(8,128)S(1)}, f32[1,20480]{1,0:T(1,128)S(1)}, f32[1,20480]{1,0:T(1,128)S(1)}) custom-call(s32[1,16384]{1,0:T(1,128)} %bitcast.2, f32[3,16384]{1,0:T(4,128)} %coords_in.1, s32[1,16384]{1,0:T(1,128)} %bitcast.3, bf16[128,2048]{1,0:T(8,128)(2,1)} %fields_in.1), custom_call_target="tpu_custom_call" | custom-call | tf_op jit(solution)/shard_map/pallas_call | solution.py:480
  35.3 4.3 %shard_map.47 = f32[4,16384]{1,0:T(4,128)} custom-call(f32[20,32,128]{2,1,0:T(8,128)S(1)} %get-tuple-element.8.values_ref, f32[1,20480]{1,0:T(1,128)S(1)} %get-tuple-element.9.row_ref, f32[1,20480]{1,0:T(1,128)S(1)} %get-tuple-element.10.lane_ref), custom_call_target="tpu_custom_call" | custom-call | tf_op jit(solution)/shard_map/pallas_call | solution.py:507

commit v3 on v2

--- a/solution.py
+++ b/solution.py
@@ -16,6 +16,9 @@
 BATCH = 16
 SWEEP = 32
 SPAN = 1024.0
+COARSE = 256.0
+FINE = 64.0
+LEAD = 1
 
 gll_points = np.array(
     [
@@ -95,12 +98,12 @@
 
 def offset_bits(sizes, group, j):
     rest = sizes[0] * sizes[1] * sizes[2] // (2 * GROUP)
+    hot = (group + rest - LEAD - 1) // rest % 2
     if isinstance(group, int):
-        hot = int(1 <= group <= rest)
-        which = group - 1 if hot else max(group - rest, 0)
+        cold = min(group, max(group - rest, LEAD))
     else:
-        hot = (group + rest - 1) // rest % 2
-        which = hot * (group - 1) + (1 - hot) * jnp.maximum(group - rest, 0)
+        cold = jnp.minimum(group, jnp.maximum(group - rest, LEAD))
+    which = hot * (group - LEAD - 1) + (1 - hot) * cold
     width = sum((n - 1).bit_length() for n in sizes)
     return [j % 2, j // 2 % 2, hot] + [which // 2**k % 2 for k in range(width - 3)]
 
@@ -182,11 +185,13 @@
             row_hots.append(jnp.where(row_ids == spread(row_ref[:, at], rows), one, zero))
             here = lane_ids == spread(lane_ref[:, at], spots)
             parts = []
+            slot = slot_ref[:, at]
+            digits = [slot & 7, (slot >> 3) & 7, slot >> 6]
             for v in range(3):
-                value = coords_ref[v : v + 1, at]
-                high = value.astype(BF16).astype(F32)
-                parts += [high, value - high]
-            parts.append(slot_ref[:, at].astype(F32))
+                value = coords_ref[v : v + 1, at] * COARSE
+                high = jnp.floor(value)
+                low = jnp.floor((value - high) * FINE)
+                parts += [high, low + (digits[v] * int(FINE) - int(COARSE)).astype(F32)]
             lane_parts.append(jnp.concatenate([jnp.where(here, spread(part, spots), zero) for part in parts], axis=0))
         acc_ref[...] += lax.dot_general(
             jnp.concatenate(lane_parts, axis=1),
@@ -217,13 +222,16 @@
             stacked = []
             for half in range(groups // per):
                 columns = slice(half * LANES, (half + 1) * LANES)
-                pieces = []
-                for v in range(first, first + per):
+                values, slot = [], 0.0
+                for v in range(3):
                     at = 2 * v * spots + b * width
-                    piece = acc_ref[at : at + width, columns]
-                    if v < 3:
-                        piece = piece + acc_ref[at + spots : at + spots + width, columns]
-                    pieces.append(piece)
+                    high = acc_ref[at : at + width, columns]
+                    low = acc_ref[at + spots : at + spots + width, columns] + COARSE
+                    digit = jnp.floor(low * (1.0 / FINE))
+                    values.append((high + (low - digit * FINE + 0.5) * (1.0 / FINE)) * (1.0 / COARSE))
+                    slot = slot + digit * float(8**v)
+                values.append(slot)
+                pieces = values[first : first + per]
                 stacked += exchange(pieces, count)
             flipped = jnp.concatenate(stacked, axis=0).T
             for v in range(first, first + per):
@@ -367,14 +375,11 @@
     )
     pl.semaphore_wait(barrier, count - 1)
     assemble(count, blocks, acc_ref, send_ref, recv_ref)
-    for group, j in others:
+    groups = count // GROUP
+    early = [g for g in range(groups) if g == 0 or offset_bits(sizes, g, 0)[2]]
+    for group, j in sorted(others, key=lambda at: at[0] not in early):
         outward(group, j).start()
-    groups = count // GROUP
     pickers = [picker_even, picker_odd]
-
-    def reply(group, skip):
-        for j in range(skip, GROUP):
-            backward(group, j).start()
 
     def serve(group):
         first = group * GROUP
@@ -383,22 +388,23 @@
             combine(blocks, block, first, recv_ref, turned_ref, nodes_ref, values_ref, pickers[block % 2])
 
     def body(group, _):
-        @pl.when(group > 1)
-        def _():
-            backward(group - 1, 0).start()
-
         @pl.when(group > 0)
         def _():
-            reply(group - 1, 1)
             outward(group, 0).wait_recv()
 
         for j in range(1, GROUP):
             outward(group, j).wait_recv()
         serve(group)
+        for j in range(1, GROUP):
+            backward(group, j).start()
+
+        @pl.when(group > 0)
+        def _():
+            backward(group, 0).start()
+
         return 0
 
     lax.fori_loop(0, groups, body, 0)
-    reply(groups - 1, 0)
     back_ref[:, 0:1] = values_ref[:, 0:1]
 
     def finish(group, skip):
@@ -490,7 +496,7 @@
             pltpu.VMEM((64, LANES), F32),
             pltpu.VMEM((2 * depth, 4 * elements), BF16),
             pltpu.VMEM((LANES, elements), F32),
-            pltpu.VMEM((7 * spots, rows), F32),
+            pltpu.VMEM((6 * spots, rows), F32),
         ]
         + [buffer] * 3
         + [picker] * 2

time: 39.7 us -> 38.5 us (0.970)
  Pallas kernels: 39.6 us -> 38.4 us
    pallas_call x1, Pallas kernels: 35.3 us -> 34.1 us  [local(): call(functools.partial(sample_kernel, sizes, blocks), [HBM] * 4, (layout,...]
where the time goes in v3:
time: 38.5 us; the launch traced here: 38.4 us
  Pallas kernels  38.4 us (100%)
    pallas_call x1, Pallas kernels, local(): call(functools.partial(sample_kernel, sizes, blocks), [HBM] * 4, (layout,...  34.1 us
    pallas_call x1, Pallas kernels, local(): call(functools.partial(return_kernel, blocks), [VMEM] * 3, jax.ShapeDtype...  4.3 us

profile of v3, /device:TPU:0, one launch (start us, length us, event | category | flops | bytes accessed | tf_op | source)
XLA Modules:
  0.0 38.4 jit_solution(14221195976533443119)
XLA Ops:
  0.0 34.1 %shard_map.46 = (f32[20,32,128]{2,1,0:T(8,128)S(1)}, f32[1,20480]{1,0:T(1,128)S(1)}, f32[1,20480]{1,0:T(1,128)S(1)}) custom-call(s32[1,16384]{1,0:T(1,128)} %bitcast.2, f32[3,16384]{1,0:T(4,128)} %coords_in.1, s32[1,16384]{1,0:T(1,128)} %bitcast.3, bf16[128,2048]{1,0:T(8,128)(2,1)} %fields_in.1), custom_call_target="tpu_custom_call" | custom-call | tf_op jit(solution)/shard_map/pallas_call | solution.py:486
  34.1 4.3 %shard_map.47 = f32[4,16384]{1,0:T(4,128)} custom-call(f32[20,32,128]{2,1,0:T(8,128)S(1)} %get-tuple-element.8.values_ref, f32[1,20480]{1,0:T(1,128)S(1)} %get-tuple-element.9.row_ref, f32[1,20480]{1,0:T(1,128)S(1)} %get-tuple-element.10.lane_ref), custom_call_target="tpu_custom_call" | custom-call | tf_op jit(solution)/shard_map/pallas_call | solution.py:513

commit v4 on v3

--- a/solution.py
+++ b/solution.py
@@ -18,7 +18,6 @@
 SPAN = 1024.0
 COARSE = 256.0
 FINE = 64.0
-LEAD = 1
 
 gll_points = np.array(
     [
@@ -97,13 +96,13 @@
 
 
 def offset_bits(sizes, group, j):
-    rest = sizes[0] * sizes[1] * sizes[2] // (2 * GROUP)
-    hot = (group + rest - LEAD - 1) // rest % 2
-    if isinstance(group, int):
-        cold = min(group, max(group - rest, LEAD))
-    else:
-        cold = jnp.minimum(group, jnp.maximum(group - rest, LEAD))
-    which = hot * (group - LEAD - 1) + (1 - hot) * cold
+    groups = sizes[0] * sizes[1] * sizes[2] // GROUP
+    last = group // (groups - 2)
+    least = min if isinstance(group, int) else jnp.minimum
+    first = 1 - least(group, 1)
+    middle = 1 - last - first
+    hot = middle * (group % 2) + last * (groups - 1 - group)
+    which = middle * (group // 2 + 1) + last * (group - (groups - 2))
     width = sum((n - 1).bit_length() for n in sizes)
     return [j % 2, j // 2 % 2, hot] + [which // 2**k % 2 for k in range(width - 3)]
 
@@ -376,8 +375,7 @@
     pl.semaphore_wait(barrier, count - 1)
     assemble(count, blocks, acc_ref, send_ref, recv_ref)
     groups = count // GROUP
-    early = [g for g in range(groups) if g == 0 or offset_bits(sizes, g, 0)[2]]
-    for group, j in sorted(others, key=lambda at: at[0] not in early):
+    for group, j in others:
         outward(group, j).start()
     pickers = [picker_even, picker_odd]
 

time: 38.5 us -> 37.1 us (0.964)
  Pallas kernels: 38.4 us -> 37 us
    pallas_call x1, Pallas kernels: 34.1 us -> 32.7 us  [local(): call(functools.partial(sample_kernel, sizes, blocks), [HBM] * 4, (layout,...]
where the time goes in v4:
time: 37.1 us; the launch traced here: 37 us
  Pallas kernels  37 us (100%)
    pallas_call x1, Pallas kernels, local(): call(functools.partial(sample_kernel, sizes, blocks), [HBM] * 4, (layout,...  32.7 us
    pallas_call x1, Pallas kernels, local(): call(functools.partial(return_kernel, blocks), [VMEM] * 3, jax.ShapeDtype...  4.3 us

profile of v4, /device:TPU:0, one launch (start us, length us, event | category | flops | bytes accessed | tf_op | source)
XLA Modules:
  0.0 37.0 jit_solution(1942537525344126699)
XLA Ops:
  0.0 32.7 %shard_map.46 = (f32[20,32,128]{2,1,0:T(8,128)S(1)}, f32[1,20480]{1,0:T(1,128)S(1)}, f32[1,20480]{1,0:T(1,128)S(1)}) custom-call(s32[1,16384]{1,0:T(1,128)} %bitcast.2, f32[3,16384]{1,0:T(4,128)} %coords_in.1, s32[1,16384]{1,0:T(1,128)} %bitcast.3, bf16[128,2048]{1,0:T(8,128)(2,1)} %fields_in.1), custom_call_target="tpu_custom_call" | custom-call | tf_op jit(solution)/shard_map/pallas_call | solution.py:484
  32.7 4.3 %shard_map.47 = f32[4,16384]{1,0:T(4,128)} custom-call(f32[20,32,128]{2,1,0:T(8,128)S(1)} %get-tuple-element.8.values_ref, f32[1,20480]{1,0:T(1,128)S(1)} %get-tuple-element.9.row_ref, f32[1,20480]{1,0:T(1,128)S(1)} %get-tuple-element.10.lane_ref), custom_call_target="tpu_custom_call" | custom-call | tf_op jit(solution)/shard_map/pallas_call | solution.py:511

commit v5 on v4

--- a/solution.py
+++ b/solution.py
@@ -116,7 +116,7 @@
     return tuple(at)
 
 
-def place_batch(count, step, targets, carry, rank_ref, prefix_ref, row_ref, lane_ref):
+def place_batch(count, step, targets, carry, rank_ref, prefix_ref, row_ref, lane_ref, next_ref):
     group = min(BATCH, max(1, CHUNK // count))
     groups, width, _ = splits(count)
     for inner in range(BATCH // group):
@@ -137,8 +137,13 @@
             position = found - peer * SPAN
             part = jnp.floor(position * (1.0 / width))
             block = jnp.floor(part * (1.0 / groups))
-            lane_ref[:, at] = position - (part - block) * width
-            row_ref[:, at] = (part - block * groups) * count + peer
+            lane = position - (part - block) * width
+            row = (part - block * groups) * count + peer
+            lane_ref[:, at] = lane
+            row_ref[:, at] = row
+            here = slice((inner * group + g) * CHUNK, (inner * group + g + 1) * CHUNK)
+            next_ref[0, :, here] = row
+            next_ref[1, :, here] = lane
             carry = carry + piece[:, CHUNK:]
     return carry
 
@@ -157,6 +162,8 @@
     flip_ref,
     row_ref,
     lane_ref,
+    next_ref,
+    now_ref,
     acc_ref,
 ):
     count = sizes[0] * sizes[1] * sizes[2]
@@ -175,14 +182,15 @@
     acc_ref[...] = jnp.zeros_like(acc_ref)
 
     def put(step, carry):
-        return place_batch(count, step, targets, carry, rank_ref, prefix_ref, row_ref, lane_ref)
+        return place_batch(count, step, targets, carry, rank_ref, prefix_ref, row_ref, lane_ref, next_ref)
 
     def scatter(step):
         row_hots, lane_parts = [], []
         for g in range(BATCH):
             at = pl.ds(pl.multiple_of((step * BATCH + g) * CHUNK, CHUNK), CHUNK)
-            row_hots.append(jnp.where(row_ids == spread(row_ref[:, at], rows), one, zero))
-            here = lane_ids == spread(lane_ref[:, at], spots)
+            here = slice(g * CHUNK, (g + 1) * CHUNK)
+            row_hots.append(jnp.where(row_ids == spread(now_ref[0, :, here], rows), one, zero))
+            inside = lane_ids == spread(now_ref[1, :, here], spots)
             parts = []
             slot = slot_ref[:, at]
             digits = [slot & 7, (slot >> 3) & 7, slot >> 6]
@@ -191,7 +199,7 @@
                 high = jnp.floor(value)
                 low = jnp.floor((value - high) * FINE)
                 parts += [high, low + (digits[v] * int(FINE) - int(COARSE)).astype(F32)]
-            lane_parts.append(jnp.concatenate([jnp.where(here, spread(part, spots), zero) for part in parts], axis=0))
+            lane_parts.append(jnp.concatenate([jnp.where(inside, spread(part, spots), zero) for part in parts], axis=0))
         acc_ref[...] += lax.dot_general(
             jnp.concatenate(lane_parts, axis=1),
             jnp.concatenate(row_hots, axis=1),
@@ -202,12 +210,15 @@
             turn(step * (tiles // steps) + tile, fields_ref, turned_ref, flip_ref)
 
     def both(step, carry):
+        carry = put(step + 1, carry)
         scatter(step)
-        return put(step + 1, carry)
+        now_ref[...] = next_ref[...]
+        return carry
 
     rank_ref[:, probes:] = jnp.zeros((1, rank_ref.shape[1] - probes), jnp.int32)
     loads[0].wait()
     carry = put(0, steps_of.astype(F32) * SPAN)
+    now_ref[...] = next_ref[...]
     for load in loads[1:]:
         load.wait()
     lax.fori_loop(0, steps, both, carry)
@@ -298,6 +309,8 @@
     nodes_ref,
     turned_ref,
     flip_ref,
+    next_ref,
+    now_ref,
     acc_ref,
     send_ref,
     recv_ref,
@@ -370,6 +383,8 @@
         flip_ref,
         row_ref,
         lane_ref,
+        next_ref,
+        now_ref,
         acc_ref,
     )
     pl.semaphore_wait(barrier, count - 1)
@@ -494,6 +509,8 @@
             pltpu.VMEM((64, LANES), F32),
             pltpu.VMEM((2 * depth, 4 * elements), BF16),
             pltpu.VMEM((LANES, elements), F32),
+            pltpu.VMEM((2, 1, BATCH * CHUNK), F32),
+            pltpu.VMEM((2, 1, BATCH * CHUNK), F32),
             pltpu.VMEM((6 * spots, rows), F32),
         ]
         + [buffer] * 3

time: 37.1 us -> 37.2 us (level)
  no operation moved by 1% of the time
where the time goes in v5:
time: 37.2 us; the launch traced here: 37 us
  Pallas kernels  37 us (99%)
    pallas_call x1, Pallas kernels, local(): call(functools.partial(sample_kernel, sizes, blocks), [HBM] * 4, (layout,...  32.7 us
    pallas_call x1, Pallas kernels, local(): call(functools.partial(return_kernel, blocks), [VMEM] * 3, jax.ShapeDtype...  4.3 us

profile of v5, /device:TPU:0, one launch (start us, length us, event | category | flops | bytes accessed | tf_op | source)
XLA Modules:
  0.0 37.0 jit_solution(2151230587704705735)
XLA Ops:
  0.0 32.7 %shard_map.46 = (f32[20,32,128]{2,1,0:T(8,128)S(1)}, f32[1,20480]{1,0:T(1,128)S(1)}, f32[1,20480]{1,0:T(1,128)S(1)}) custom-call(s32[1,16384]{1,0:T(1,128)} %bitcast.2, f32[3,16384]{1,0:T(4,128)} %coords_in.1, s32[1,16384]{1,0:T(1,128)} %bitcast.3, bf16[128,2048]{1,0:T(8,128)(2,1)} %fields_in.1), custom_call_target="tpu_custom_call" | custom-call | tf_op jit(solution)/shard_map/pallas_call | solution.py:499
  32.7 4.3 %shard_map.47 = f32[4,16384]{1,0:T(4,128)} custom-call(f32[20,32,128]{2,1,0:T(8,128)S(1)} %get-tuple-element.8.values_ref, f32[1,20480]{1,0:T(1,128)S(1)} %get-tuple-element.9.row_ref, f32[1,20480]{1,0:T(1,128)S(1)} %get-tuple-element.10.lane_ref), custom_call_target="tpu_custom_call" | custom-call | tf_op jit(solution)/shard_map/pallas_call | solution.py:528
